TPU v7x, 32 devices: a whole 2x2x4 slice. The times are simulated.
32 devices in a mesh: my: 8 (over z, y), mx: 4 (over x, core).
Axes of the slice: x: 2, y: 2, z: 4, core: 2. Of those that a mesh axis runs over, the one named last changes fastest.
Arguments:
- x_in: bfloat16 [192, 5120], P(None, 'mx')
- seq_lens: int32 [192], P('mx')
- gain_attn: bfloat16 [5120], P('mx')
- gain_mlp: bfloat16 [5120], P('mx')
- w_q: bfloat16 [5120, 5120], P('mx', 'my')
- b_q: bfloat16 [5120], P('my')
- w_k: bfloat16 [5120, 1024], P('mx', 'my')
- b_k: bfloat16 [1024], P('my')
- w_v: bfloat16 [5120, 1024], P('mx', 'my')
- b_v: bfloat16 [1024], P('my')
- w_o: bfloat16 [5120, 5120], P('my', 'mx')
- w_gate: bfloat16 [5120, 27392], P('mx', 'my')
- w_up: bfloat16 [5120, 27392], P('mx', 'my')
- w_down: bfloat16 [27392, 5120], P('my', 'mx')
- k_cache: bfloat16 [192, 384, 8, 128], P('mx', None, 'my')
- v_cache: bfloat16 [192, 384, 8, 128], P('mx', None, 'my')
Outputs:
- output 1: bfloat16 [192, 5120], P(None, 'mx')
- output 2: bfloat16 [192, 384, 8, 128], P('mx', None, 'my')
- output 3: bfloat16 [192, 384, 8, 128], P('mx', None, 'my')
All inputs are finite; a program needn't handle non-finite values.
Results may differ from a plain program's by a relative error of at most 0.0177699.
Values are sent between devices in bfloat16 or wider.
A program may use at most 1 GiB of HBM per device.

v0:
```python
import functools
import types

import jax
import jax.numpy as jnp
import numpy as np
from jax import lax
from jax.experimental import pallas as pl
from jax.experimental.pallas import tpu as pltpu
from jax.sharding import PartitionSpec as P

HEAD = 128
NORM_EPS = 1e-6
ROPE_THETA = 1000000.0
MESH = pl.DeviceIdType.MESH
CHUNK = 512
TILE = 256
DIRECT = 2
ROWS = 64
LAG_B, LAG_C, LAG_D, LAG_E, LAG_M, LAG_F = 1, 4, 7, 8, 3, 9
VMEM_LIMIT = 67043328
MLP_LIMIT = 48 * 1024 * 1024
ATTN_LIMIT = 14 * 1024 * 1024
QKV_LIMIT = 8 * 1024 * 1024


def rcopy(src, dst, send_sem, recv_sem, dev):
    return pltpu.make_async_remote_copy(src_ref=src, dst_ref=dst, send_sem=send_sem, recv_sem=recv_sem, device_id=dev, device_id_type=MESH)


def pinned(x):
    return pltpu.with_memory_space_constraint(x, pltpu.HBM)


def lane_ids():
    return lax.broadcasted_iota(jnp.int32, (8, 128), 1)


def pack_column(blocks):
    tile = jnp.zeros((8, 128), jnp.float32)
    lanes = lane_ids()
    for k, block in enumerate(blocks):
        tile = jnp.where(lanes == k, block, tile)
    return tile


def unpack_column(tile, k):
    return jnp.sum(jnp.where(lane_ids() == k, tile, 0.0), axis=1, keepdims=True)


def qkv_kernel(hidden, x_hbm, gain_hbm, wq_hbm, wk_hbm, wv_hbm, out_ref, gain_ref, x_v, wq_v, wk_v, wv_v, st_own, st_in, nrm, pp, dr, own, xs, xr, ld_sem, send_sem, st_sem, d_sem, x_sem):
    mx = lax.axis_index("mx")
    xi, ci = mx // 2, mx % 2
    partner, xpeer = 2 * xi + (1 - ci), 2 * (1 - xi) + ci
    loads = [pltpu.make_async_copy(s, d, ld_sem.at[i]) for i, (s, d) in enumerate([(x_hbm, x_v), (gain_hbm, gain_ref), (wq_hbm, wq_v), (wk_hbm, wk_v), (wv_hbm, wv_v)])]
    for ld in loads:
        ld.start()
    barrier = pltpu.get_barrier_semaphore()
    for d in range(1, 4):
        pl.semaphore_signal(barrier, inc=1, device_id={"mx": (mx + d) % 4}, device_id_type=MESH)
    pl.semaphore_wait(barrier, 3)

    rows = x_v.shape[0]
    loads[0].wait()
    blocks = []
    for k in range(rows // 8):
        v = x_v[8 * k:8 * k + 8, :].astype(jnp.float32)
        blocks.append(jnp.sum(v * v, axis=1, keepdims=True))
    tile = pack_column(blocks)
    st_own[...] = tile
    st_in[mx] = tile
    for d in range(1, 4):
        rcopy(st_own, st_in.at[mx], send_sem.at[0], st_sem, {"mx": (mx + d) % 4}).start()
    for ld in loads[1:]:
        ld.wait()
    rcopy(st_in.at[pl.ds(0, 3)], st_in.at[pl.ds(0, 3)], send_sem.at[0], st_sem, {"mx": partner}).wait()
    total = st_in[0] + st_in[1] + st_in[2] + st_in[3]
    scale = lax.rsqrt(total / hidden + NORM_EPS)
    gain = gain_ref[...].astype(jnp.float32).reshape(1, x_v.shape[1])
    for k in range(0, rows // 8, 2):
        col = jnp.concatenate([unpack_column(scale, k), unpack_column(scale, k + 1)], axis=0)
        nrm[8 * k:8 * k + 16, :] = (x_v[8 * k:8 * k + 16, :].astype(jnp.float32) * col * gain).astype(jnp.bfloat16)

    lhs = nrm[...]
    part = rows // 4
    width = out_ref.shape[1]
    offs = [0, wq_v.shape[1], wq_v.shape[1] + wk_v.shape[1]]
    pieces = [(w, c0, min(c0 + TILE, w.shape[1]), off) for w, off in zip((wq_v, wk_v, wv_v), offs) for c0 in range(0, w.shape[1], TILE)]
    cut = 2 * TILE
    parts = ((0, cut), (cut, width))

    def swap(i):
        cols = pl.ds(parts[i][0], parts[i][1] - parts[i][0])
        return rcopy(pp.at[1 - ci, :, :, cols], dr.at[:, :, cols], send_sem.at[1], d_sem.at[i], {"mx": partner})

    def cross(i):
        cols = pl.ds(parts[i][0], parts[i][1] - parts[i][0])
        return rcopy(xs.at[:, cols], xr.at[:, cols], send_sem.at[2], x_sem.at[i], {"mx": xpeer})

    for i, (lo, hi) in enumerate(parts):
        for w, c0, c1, off in pieces:
            if lo <= off + c0 < hi:
                r = jnp.dot(lhs, w[:, c0:c1], preferred_element_type=jnp.float32).astype(jnp.bfloat16)
                for m in range(4):
                    pp[m % 2, m // 2, :, off + c0:off + c1] = r[m * part:(m + 1) * part]
        swap(i).start()
    for i, (lo, hi) in enumerate(parts):
        swap(i).wait_recv()
        xs[:, lo:hi] = (pp[ci, 1 - xi, :, lo:hi].astype(jnp.float32) + dr[1 - xi, :, lo:hi].astype(jnp.float32)).astype(jnp.bfloat16)
        cross(i).start()
        own[:, lo:hi] = pp[ci, xi, :, lo:hi].astype(jnp.float32) + dr[xi, :, lo:hi].astype(jnp.float32)
    for i, (lo, hi) in enumerate(parts):
        cross(i).wait_recv()
        out_ref[:, lo:hi] = own[:, lo:hi] + xr[:, lo:hi].astype(jnp.float32)
    for i in range(2):
        swap(i).wait_send()
        cross(i).wait_send()


def qkv_call(x_in, gain, w_q, w_k, w_v, hidden):
    rows, cols = x_in.shape
    width = w_q.shape[1] + w_k.shape[1] + w_v.shape[1]
    bf, f32 = jnp.bfloat16, jnp.float32
    any_spec, vmem = pl.BlockSpec(memory_space=pl.ANY), pl.BlockSpec(memory_space=pltpu.VMEM)
    part = rows // 4
    return pl.pallas_call(
        functools.partial(qkv_kernel, hidden),
        name="qkv",
        out_shape=jax.ShapeDtypeStruct((part, width), f32),
        in_specs=[any_spec] * 5,
        out_specs=vmem,
        scratch_shapes=[
            pltpu.VMEM(gain.shape, bf),
            pltpu.VMEM((rows, cols), bf), pltpu.VMEM(w_q.shape, bf), pltpu.VMEM(w_k.shape, bf), pltpu.VMEM(w_v.shape, bf),
            pltpu.VMEM((8, 128), f32), pltpu.VMEM((4, 8, 128), f32), pltpu.VMEM((rows, cols), bf),
            pltpu.VMEM((2, 2, part, width), bf), pltpu.VMEM((2, part, width), bf), pltpu.VMEM((part, width), f32),
            pltpu.VMEM((part, width), bf), pltpu.VMEM((part, width), bf),
            pltpu.SemaphoreType.DMA((5,)), pltpu.SemaphoreType.DMA((3,)), pltpu.SemaphoreType.DMA, pltpu.SemaphoreType.DMA((2,)), pltpu.SemaphoreType.DMA((2,)),
        ],
        compiler_params=pltpu.CompilerParams(collective_id=0, has_side_effects=True, vmem_limit_bytes=QKV_LIMIT),
        cost_estimate=pl.CostEstimate(flops=10 ** 10, bytes_accessed=3 * 10 ** 6, transcendentals=0),
    )(pinned(x_in), pinned(gain), pinned(w_q), pinned(w_k), pinned(w_v))


def mlp_kernel(hidden, x_v, gain_ref, attn_ref, wo_v, wg_hbm, wu_hbm, wd_hbm, ag2,
               wg_v, wu_v, wd_v, attn_v, p1, yb1, zs1, zb1, mp, ag1, st_own, st_in, st_sum, st_all, h2,
               pp, dr, own, xs, xr, act, dacc, p2, yb2, zs2, zb2, mo, eye,
               ld_sem, send_sem, at_sem, st_sem, sg_sem, ysem1, zsem1, agz1, agy1, ysem2, zsem2, agz2, agy2, d_sem, x_sem, ax_sem, ad_sem, af_sem):
    my, mx = lax.axis_index("my"), lax.axis_index("mx")
    n_my = 8
    xi, ci = mx // 2, mx % 2
    zi, yi = my // 2, my % 2
    partner, xpeer = 2 * xi + (1 - ci), 2 * (1 - xi) + ci
    core_dev, x_dev = {"mx": partner}, {"mx": xpeer}
    n_h = h2.shape[0]
    ff = wg_hbm.shape[0]
    n_j = pl.cdiv(ff, CHUNK)
    steps = n_h * n_j
    half = x_v.shape[1] // 2
    brows = attn_ref.shape[0]
    f32, bf = jnp.float32, jnp.bfloat16

    n_k = wg_v.shape[0]
    tiles = [(src.at[:, pl.ds(TILE * k, TILE)], dst.at[k, pl.ds(0, ff)]) for src, dst in ((wg_hbm, wg_v), (wu_hbm, wu_v)) for k in range(n_k)]
    loads = [pltpu.make_async_copy(s, d, ld_sem.at[i]) for i, (s, d) in enumerate(tiles + [(wd_hbm, wd_v.at[pl.ds(0, ff)])])]
    for ld in loads:
        ld.start()
    barrier = pltpu.get_barrier_semaphore()
    for d in range(1, 4):
        pl.semaphore_signal(barrier, inc=1, device_id={"mx": (mx + d) % 4}, device_id_type=MESH)
    for d in range(1, n_my):
        pl.semaphore_signal(barrier, inc=1, device_id={"my": (my + d) % n_my}, device_id_type=MESH)
    pl.semaphore_wait(barrier, 3 + n_my - 1)

    mine = pl.ds(pl.multiple_of(mx * 16, 16), 16)
    for h in range(n_h):
        for d in range(1, 4):
            rcopy(attn_ref.at[pl.ds(16 * h, 16)], attn_v.at[h, mine], send_sem.at[0], at_sem.at[h], {"mx": (mx + d) % 4}).start()
    for h in range(n_h):
        attn_v[h, mine, :] = attn_ref[16 * h:16 * h + 16, :]
    dacc[...] = jnp.zeros_like(dacc)
    wd_v[ff:, :] = jnp.zeros((wd_v.shape[0] - ff, wd_v.shape[1]), bf)
    for w in (wg_v, wu_v):
        for k in range(n_k):
            w[k, ff:, :] = jnp.zeros((w.shape[1] - ff, TILE), bf)
    eye[...] = (lax.broadcasted_iota(jnp.int32, (TILE, TILE), 0) == lax.broadcasted_iota(jnp.int32, (TILE, TILE), 1)).astype(f32).astype(bf)

    zs = (3 - zi, (zi + 2) % 4, zi + 1 - 2 * (zi % 2), zi)
    peers = [2 * z + y for z in zs for y in (1 - yi, yi)][:-1]
    y_peer = 2 * zi + 1 - yi
    y_dev = {"my": y_peer}
    z_devs = [{"my": 2 * z + yi} for z in zs[:3]]

    def project(h):
        gathered = attn_v.at[h, pl.ds(0, 48)]
        rcopy(gathered, gathered, send_sem.at[0], at_sem.at[h], core_dev).wait_recv()
        for y in range(2):
            r = jnp.dot(attn_v[h], wo_v[:, y * half:(y + 1) * half], preferred_element_type=f32).astype(bf)
            for z in range(4):
                p1[h, 2 * z + y] = r[16 * z:16 * z + 16]

    parts = ((0, TILE), (TILE, half))
    spans = [pl.ds(lo, hi - lo) for lo, hi in parts]

    def rs_start(r, h):
        for i, cols in enumerate(spans):
            for k, z in enumerate(zs):
                rcopy(r.part.at[h, 2 * z + 1 - yi, :, cols], r.ybuf.at[h, k, :, cols], send_sem.at[r.sem], r.ysem.at[h, i, k], y_dev).start()

    def wait_y(r, h, i, k):
        got = r.ybuf.at[h, k, :, spans[i]]
        rcopy(got, got, send_sem.at[r.sem], r.ysem.at[h, i, k], y_dev).wait_recv()

    def rs_mid(r, h):
        for i, (lo, hi) in enumerate(parts):
            for k in range(3):
                wait_y(r, h, i, k)
                r.zsend[h, k, :, lo:hi] = (r.part[h, 2 * zs[k] + yi, :, lo:hi].astype(f32) + r.ybuf[h, k, :, lo:hi].astype(f32)).astype(bf)
                rcopy(r.zsend.at[h, k, :, spans[i]], r.zbuf.at[h, k, :, spans[i]], send_sem.at[r.sem + 1], r.zsem.at[h, i], z_devs[k]).start()

    def rs_fin(r, h, i, base):
        lo, hi = parts[i]
        wait_y(r, h, i, 3)
        got = r.zbuf.at[h, :, :, spans[i]]
        rcopy(got, got, send_sem.at[r.sem + 1], r.zsem.at[h, i], y_dev).wait_recv()
        total = r.part[h, my, :, lo:hi].astype(f32) + r.ybuf[h, 3, :, lo:hi].astype(f32)
        for k in range(3):
            total += r.zbuf[h, k, :, lo:hi].astype(f32)
        return (base + total).astype(bf)

    def ag_start(r, h, i, val):
        lo, hi = parts[i]
        r.piece[h, :, lo:hi] = val
        r.all[h, my, :, lo:hi] = val
        src, dst = r.piece.at[h, :, spans[i]], r.all.at[h, my, :, spans[i]]
        for k in range(3):
            rcopy(src, dst, send_sem.at[r.sem + 2], r.agz.at[h, i, k], z_devs[k]).start()
        rcopy(src, dst, send_sem.at[r.sem + 2], r.agy.at[h, i], y_dev).start()

    def ag_mid(r, h):
        for i in range(2):
            for k in (2, 1, 0):
                got = r.all.at[h, 2 * zs[k] + yi, :, spans[i]]
                rcopy(got, got, send_sem.at[r.sem + 2], r.agz.at[h, i, k], y_dev).wait_recv()
                rcopy(got, got, send_sem.at[r.sem + 2], r.agy.at[h, i], y_dev).start()

    def ag_fin(r, h):
        for i in range(2):
            four = r.all.at[h, pl.ds(0, 4), :, spans[i]]
            rcopy(four, four, send_sem.at[r.sem + 2], r.agy.at[h, i], y_dev).wait_recv()

    one = types.SimpleNamespace(part=p1, ybuf=yb1, zsend=zs1, zbuf=zb1, piece=mp, all=ag1, ysem=ysem1, zsem=zsem1, agz=agz1, agy=agy1, sem=9)
    two = types.SimpleNamespace(part=p2, ybuf=yb2, zsend=zs2, zbuf=zb2, piece=mo, all=ag2, ysem=ysem2, zsem=zsem2, agz=agz2, agy=agy2, sem=12)

    def rs1_finish(h):
        r0 = pl.multiple_of(zi * brows + h * 16, 16)
        ss = jnp.zeros((16, 1), f32)
        for i, (lo, hi) in enumerate(parts):
            base = x_v[pl.ds(r0, 16), pl.ds(pl.multiple_of(yi * half + lo, 128), hi - lo)].astype(f32)
            m = rs_fin(one, h, i, base)
            ag_start(one, h, i, m)
            m = m.astype(f32)
            ss += jnp.sum(m * m, axis=1, keepdims=True)
        tile = pack_column([ss[:8], ss[8:]])
        st_own[h] = tile
        st_in[h, mx] = tile
        for d in range(1, 4):
            rcopy(st_own.at[h], st_in.at[h, mx], send_sem.at[3], st_sem.at[h], {"mx": (mx + d) % 4}).start()

    def stat_gather(h):
        three = st_in.at[h, pl.ds(0, 3)]
        rcopy(three, three, send_sem.at[3], st_sem.at[h], core_dev).wait_recv()
        total = st_in[h, 0] + st_in[h, 1] + st_in[h, 2] + st_in[h, 3]
        st_sum[h] = total
        st_all[h, my] = total
        for peer in peers:
            rcopy(st_sum.at[h], st_all.at[h, my], send_sem.at[1], sg_sem.at[h], {"my": peer}).start()

    def norm(h):
        seven = st_all.at[h, pl.ds(0, n_my - 1)]
        rcopy(seven, seven, send_sem.at[1], sg_sem.at[h], y_dev).wait_recv()
        ag_fin(one, h)
        for z in range(4):
            scale = lax.rsqrt((st_all[h, 2 * z] + st_all[h, 2 * z + 1]) / hidden + NORM_EPS)
            col = jnp.concatenate([unpack_column(scale, 0), unpack_column(scale, 1)], axis=0)
            for y in range(2):
                gain = gain_ref[pl.ds(y * half, half)].astype(f32).reshape(1, half)
                h2[h, 16 * z:16 * z + 16, y * half:(y + 1) * half] = (ag1[h, 2 * z + y].astype(f32) * col * gain).astype(bf)

    def transpose(i, carry):
        rows = pl.ds(pl.multiple_of(i * TILE, TILE), TILE)
        for k in range(n_k):
            flipped = [lax.dot_general(eye[...], w[k, rows, :], (((1,), (1,)), ((), ())), preferred_element_type=f32).astype(bf) for w in (wg_v, wu_v)]
            for w, val in zip((wg_v, wu_v), flipped):
                w[k, rows, :] = val
        return carry

    def stage_a(s):
        h, j = s // n_j, s % n_j
        lhs = h2[h]
        for i, w in enumerate((wg_v, wu_v)):
            cols = []
            for n in range(CHUNK // TILE):
                rows = pl.ds(pl.multiple_of(j * CHUNK + n * TILE, TILE), TILE)
                acc = jnp.dot(lhs[:, :TILE], w[0, rows, :], preferred_element_type=f32)
                for k in range(1, n_k):
                    acc += jnp.dot(lhs[:, TILE * k:TILE * (k + 1)], w[k, rows, :], preferred_element_type=f32)
                cols.append(acc.astype(bf))
            val = jnp.concatenate(cols, axis=1)
            for m in range(4):
                pp[s, m % 2, m // 2, :, i * CHUNK:(i + 1) * CHUNK] = val[16 * m:16 * m + 16]
        rcopy(pp.at[s, 1 - ci], dr.at[s], send_sem.at[4], d_sem.at[s], core_dev).start()

    def stage_b(s):
        rcopy(pp.at[s, 1 - ci], dr.at[s], send_sem.at[4], d_sem.at[s], core_dev).wait_recv()
        xs[s] = (pp[s, ci, 1 - xi].astype(f32) + dr[s, 1 - xi].astype(f32)).astype(bf)
        rcopy(xs.at[s], xr.at[s], send_sem.at[5], x_sem.at[s], x_dev).start()
        own[s] = pp[s, ci, xi].astype(f32) + dr[s, xi].astype(f32)

    def stage_c(s):
        rcopy(xs.at[s], xr.at[s], send_sem.at[5], x_sem.at[s], x_dev).wait_recv()
        g = own[s, :, :CHUNK] + xr[s, :, :CHUNK].astype(f32)
        u = own[s, :, CHUNK:] + xr[s, :, CHUNK:].astype(f32)
        act[s, mx] = (jax.nn.silu(g) * u).astype(bf)
        rcopy(act.at[s, mx], act.at[s, mx], send_sem.at[6], ax_sem.at[s], x_dev).start()
        rcopy(act.at[s, mx], act.at[s, mx], send_sem.at[7], ad_sem.at[s], core_dev).start()

        @pl.when(s >= steps - DIRECT)
        def _():
            rcopy(act.at[s, mx], act.at[s, mx], send_sem.at[8], af_sem.at[s], {"mx": 2 * (1 - xi) + (1 - ci)}).start()

    def stage_d(s):
        rcopy(act.at[s, xpeer], act.at[s, xpeer], send_sem.at[6], ax_sem.at[s], x_dev).wait_recv()

        @pl.when(s < steps - DIRECT)
        def _():
            rcopy(act.at[s, xpeer], act.at[s, xpeer], send_sem.at[8], af_sem.at[s], core_dev).start()

    def stage_e(s):
        h, j = s // n_j, s % n_j
        rcopy(act.at[s, 0], act.at[s, 0], send_sem.at[7], ad_sem.at[s], core_dev).wait_recv()
        rcopy(act.at[s, 0], act.at[s, 0], send_sem.at[8], af_sem.at[s], core_dev).wait_recv()
        lhs = act[s].reshape(ROWS, CHUNK)
        dacc[h] += jnp.dot(lhs, wd_v[pl.ds(pl.multiple_of(j * CHUNK, CHUNK), CHUNK), :], preferred_element_type=f32)

    def rs2_send(h):
        for z in range(4):
            for y in range(2):
                p2[h, 2 * z + y] = dacc[h, 16 * z:16 * z + 16, y * half:(y + 1) * half].astype(bf)
        rs_start(two, h)

    def rs2_finish(h):
        for i, (lo, hi) in enumerate(parts):
            ag_start(two, h, i, rs_fin(two, h, i, mp[h, :, lo:hi].astype(f32)))

    n_t = n_j * (CHUNK // TILE)
    def flip(lo, hi):
        lax.fori_loop(lo, hi, transpose, 0)

    project(0)
    rs_start(one, 0)
    project(1)
    rs_start(one, 1)
    project(2)
    for ld in loads[:-1]:
        ld.wait()
    flip(0, 2)
    rs_mid(one, 0)
    flip(2, 5)
    rs_mid(one, 1)
    flip(5, 8)
    rs1_finish(0)
    rs_start(one, 2)
    flip(8, 10)
    rs1_finish(1)
    stat_gather(0)
    flip(10, 12)
    rs_mid(one, 2)
    ag_mid(one, 0)
    flip(12, n_t)
    stat_gather(1)
    norm(0)

    def body(t, carry):
        @pl.when(t == n_j)
        def _():
            norm(1)

        @pl.when(t == 2 * n_j)
        def _():
            norm(2)

        @pl.when(t == 1)
        def _():
            ag_mid(one, 1)

        @pl.when(t == 2)
        def _():
            rs1_finish(2)

        @pl.when(t == 5)
        def _():
            stat_gather(2)

        @pl.when(t == n_j + 1)
        def _():
            ag_mid(one, 2)

        @pl.when(t < steps)
        def _():
            stage_a(t)

        @pl.when((t >= LAG_B) & (t < steps + LAG_B))
        def _():
            stage_b(t - LAG_B)

        @pl.when((t >= LAG_C) & (t < steps + LAG_C))
        def _():
            stage_c(t - LAG_C)

        @pl.when((t >= LAG_D) & (t < steps + LAG_D))
        def _():
            stage_d(t - LAG_D)

        @pl.when(t == LAG_E)
        def _():
            loads[-1].wait()

        @pl.when(t >= LAG_E)
        def _():
            s = t - LAG_E
            stage_e(s)

            @pl.when(s % n_j == n_j - 1)
            def _():
                rs2_send(s // n_j)

        after = t - LAG_E - (n_j - 1)

        @pl.when((after >= LAG_M) & ((after - LAG_M) % n_j == 0))
        def _():
            rs_mid(two, (after - LAG_M) // n_j)

        @pl.when((after >= LAG_F) & ((after - LAG_F) % n_j == 0))
        def _():
            rs2_finish((after - LAG_F) // n_j)

        return carry

    total_t = steps + LAG_E
    lax.fori_loop(0, total_t, body, 0)
    rs_mid(two, 2)
    rs2_finish(1)
    ag_mid(two, 0)
    rs2_finish(2)
    ag_mid(two, 1)
    ag_mid(two, 2)
    for h in range(n_h):
        ag_fin(two, h)
    seven = pl.ds(0, n_my - 1)
    for k, ref in ((0, attn_v.at[:, pl.ds(0, 48)]), (1, st_all.at[:, seven]), (3, st_in.at[:, pl.ds(0, 3)]), (4, dr), (5, xs), (6, act.at[:, 0]), (7, act.at[:, 0]), (8, act.at[:, 0]),
                   (9, yb1), (10, zb1), (11, ag1.at[:, seven]), (12, yb2), (13, zb2), (14, ag2.at[:, seven])):
        rcopy(ref, ref, send_sem.at[k], at_sem.at[0], core_dev).wait_send()


def mlp_call(x_in, gain, attn, w_o, w_gate, w_up, w_down, hidden):
    rows, cols = x_in.shape
    ff = w_gate.shape[0]
    n_j = pl.cdiv(ff, CHUNK)
    n_h = rows // ROWS
    steps = n_h * n_j
    half = cols // 2
    bf, f32 = jnp.bfloat16, jnp.float32
    hbm, vmem = pl.BlockSpec(memory_space=pltpu.HBM), pl.BlockSpec(memory_space=pltpu.VMEM)
    dma = pltpu.SemaphoreType.DMA
    return pl.pallas_call(
        functools.partial(mlp_kernel, hidden),
        name="mlp",
        out_shape=jax.ShapeDtypeStruct((n_h, 8, 16, half), bf),
        in_specs=[vmem, vmem, vmem, vmem, hbm, hbm, hbm],
        out_specs=vmem,
        scratch_shapes=[
            pltpu.VMEM((cols // TILE, n_j * CHUNK, TILE), bf), pltpu.VMEM((cols // TILE, n_j * CHUNK, TILE), bf),
            pltpu.VMEM((n_j * CHUNK, cols), bf), pltpu.VMEM((n_h, 64, attn.shape[1]), bf),
            pltpu.VMEM((n_h, 8, 16, half), bf), pltpu.VMEM((n_h, 4, 16, half), bf), pltpu.VMEM((n_h, 3, 16, half), bf), pltpu.VMEM((n_h, 3, 16, half), bf), pltpu.VMEM((n_h, 16, half), bf), pltpu.VMEM((n_h, 8, 16, half), bf),
            pltpu.VMEM((n_h, 8, 128), f32), pltpu.VMEM((n_h, 4, 8, 128), f32), pltpu.VMEM((n_h, 8, 128), f32), pltpu.VMEM((n_h, 8, 8, 128), f32), pltpu.VMEM((n_h, ROWS, cols), bf),
            pltpu.VMEM((steps, 2, 2, 16, 2 * CHUNK), bf), pltpu.VMEM((steps, 2, 16, 2 * CHUNK), bf), pltpu.VMEM((steps, 16, 2 * CHUNK), f32),
            pltpu.VMEM((steps, 16, 2 * CHUNK), bf), pltpu.VMEM((steps, 16, 2 * CHUNK), bf), pltpu.VMEM((steps, 4, 16, CHUNK), bf),
            pltpu.VMEM((n_h, ROWS, cols), f32),
            pltpu.VMEM((n_h, 8, 16, half), bf), pltpu.VMEM((n_h, 4, 16, half), bf), pltpu.VMEM((n_h, 3, 16, half), bf), pltpu.VMEM((n_h, 3, 16, half), bf), pltpu.VMEM((n_h, 16, half), bf), pltpu.VMEM((TILE, TILE), bf),
            dma((1 + 2 * (cols // TILE),)), dma((15,)), dma((n_h,)), dma((n_h,)), dma((n_h,)), dma((n_h, 2, 4)), dma((n_h, 2)), dma((n_h, 2, 3)), dma((n_h, 2)), dma((n_h, 2, 4)), dma((n_h, 2)), dma((n_h, 2, 3)), dma((n_h, 2)),
            dma((steps,)), dma((steps,)), dma((steps,)), dma((steps,)), dma((steps,)),
        ],
        compiler_params=pltpu.CompilerParams(collective_id=1, has_side_effects=True, vmem_limit_bytes=MLP_LIMIT),
    )(x_in, gain, attn, w_o, pinned(w_gate), pinned(w_up), pinned(w_down))


def place_kernel(pieces_ref, out_ref):
    n_h, _, _, half = pieces_ref.shape
    for h in range(n_h):
        for z in range(4):
            for y in range(2):
                r0 = z * 16 * n_h + h * 16
                out_ref[r0:r0 + 16, y * half:(y + 1) * half] = pieces_ref[h, 2 * z + y]


def place_call(pieces, shape):
    vmem = pl.BlockSpec(memory_space=pltpu.VMEM)
    return pl.pallas_call(place_kernel, name="place", out_shape=jax.ShapeDtypeStruct(shape, pieces.dtype), in_specs=[vmem], out_specs=vmem, compiler_params=pltpu.CompilerParams(vmem_limit_bytes=4 * 1024 * 1024))(pieces)


GROUP_ROWS = 16


def attn_kernel(seq_ref, proj_ref, bq_ref, bk_ref, bv_ref, freq_ref, k_ref, v_ref, attn_ref, ko_hbm, vo_hbm, qs, kn, vn, os, pos, patch, out_sem, patch_sem):
    f32, bf = jnp.float32, jnp.bfloat16
    rows, seq = k_ref.shape[0], k_ref.shape[1]
    heads = attn_ref.shape[1] // HEAD
    groups = rows // GROUP_ROWS
    outs = [ko_hbm, vo_hbm]

    def bulk(g):
        part = pl.ds(g * GROUP_ROWS, GROUP_ROWS)
        return [pltpu.make_async_copy(src.at[part], dst.at[part], out_sem.at[i, g]) for i, (src, dst) in enumerate(zip((k_ref, v_ref), outs))]

    for g in range(groups):
        for cp in bulk(g):
            cp.start()
    for b in range(rows):
        pos[b:b + 1, :] = jnp.full((1, HEAD), seq_ref[b], jnp.int32).astype(f32)
    angles = pos[...] * freq_ref[...]
    lower = lax.broadcasted_iota(jnp.int32, (rows, HEAD), 1) < HEAD // 2
    cos_tab = jnp.cos(angles)
    sin_tab = jnp.sin(angles)
    sin_tab = jnp.where(lower, -sin_tab, sin_tab)

    def column(c, bias_ref, k):
        bias = bias_ref[pl.ds(k * HEAD, HEAD)].astype(f32).reshape(1, HEAD)
        return proj_ref[:, c * HEAD:(c + 1) * HEAD] + bias

    def rotate(v):
        return (v * cos_tab + pltpu.roll(v, HEAD // 2, 1) * sin_tab).astype(bf).astype(f32)

    qs[...] = jnp.zeros_like(qs)
    for h in range(heads):
        qs[:, h, :] = rotate(column(h, bq_ref, h))
    kn[...] = rotate(column(heads, bk_ref, 0))
    vn[...] = column(heads + 1, bv_ref, 0).astype(bf).astype(f32)

    def slab_of(b):
        p = seq_ref[b]
        return p, pl.multiple_of((p // 16) * 16, 16)

    def body(g, carry):
        times = lax.broadcasted_iota(jnp.int32, (8, seq), 1)
        slots = lax.broadcasted_iota(jnp.int32, (16, HEAD), 0)
        scores, news, hits = [], [], []
        for r in range(GROUP_ROWS):
            b = g * GROUP_ROWS + r
            p, slab = slab_of(b)
            hit = slots == p - slab
            for i, (cache, new) in enumerate(((k_ref, kn), (v_ref, vn))):
                old = cache[b, pl.ds(slab, 16), :].astype(f32)
                patch[i, b] = jnp.where(hit, new[pl.ds(b, 1), :], old).astype(bf)
            q = qs[b]
            s = lax.dot_general(q.astype(bf), k_ref[b], (((1,), (1,)), ((), ())), preferred_element_type=f32) * HEAD ** -0.5
            s_new = jnp.sum(q * kn[pl.ds(b, 1), :], axis=1, keepdims=True) * HEAD ** -0.5
            hits.append(times == p)
            news.append(s_new)
            scores.append(jnp.where(hits[r], s_new, jnp.where(times < p, s, -jnp.inf)))
        s = jnp.concatenate(scores, axis=0)
        top = jnp.max(s, axis=1, keepdims=True)
        w = jnp.exp(s - top)
        total = jnp.sum(w, axis=1, keepdims=True)
        w_new = jnp.exp(jnp.concatenate(news, axis=0) - top).astype(bf).astype(f32)
        w = jnp.where(jnp.concatenate(hits, axis=0), 0.0, w).astype(bf)
        for r in range(GROUP_ROWS):
            b = g * GROUP_ROWS + r
            part = slice(8 * r, 8 * r + 8)
            o = jnp.dot(w[part], v_ref[b], preferred_element_type=f32) + w_new[part] * vn[pl.ds(b, 1), :]
            os[b] = o / total[part]
        return carry

    lax.fori_loop(0, groups, body, 0)
    for h in range(heads):
        attn_ref[:, h * HEAD:(h + 1) * HEAD] = os[:, h, :].astype(bf)

    def patches(b):
        slab = slab_of(b)[1]
        return [pltpu.make_async_copy(patch.at[i, b], dst.at[b, pl.ds(slab, 16)], patch_sem.at[i]) for i, dst in enumerate(outs)]

    for g in range(groups):
        for cp in bulk(g):
            cp.wait()
        for b in range(g * GROUP_ROWS, (g + 1) * GROUP_ROWS):
            for cp in patches(b):
                cp.start()
    for b in range(rows):
        for cp in patches(b):
            cp.wait()


def attn_call(seq_lens, projected, b_q, b_k, b_v, k_cache, v_cache):
    rows, seq = k_cache.shape[0], k_cache.shape[1]
    f32, bf = jnp.float32, jnp.bfloat16
    freq = (ROPE_THETA ** (-2.0 * np.arange(HEAD // 2) / HEAD)).astype(np.float32)
    freq = jnp.asarray(np.concatenate([freq, freq])[None])
    any_spec, vmem, smem = pl.BlockSpec(memory_space=pl.ANY), pl.BlockSpec(memory_space=pltpu.VMEM), pl.BlockSpec(memory_space=pltpu.SMEM)
    dma = pltpu.SemaphoreType.DMA
    cache = jax.ShapeDtypeStruct((rows, seq, HEAD), bf)
    return pl.pallas_call(
        attn_kernel,
        name="attn",
        out_shape=(jax.ShapeDtypeStruct((rows, b_q.shape[0]), bf), cache, cache),
        in_specs=[smem, vmem, vmem, vmem, vmem, vmem, vmem, vmem],
        out_specs=(vmem, any_spec, any_spec),
        scratch_shapes=[
            pltpu.VMEM((rows, 8, HEAD), f32), pltpu.VMEM((rows, HEAD), f32),
            pltpu.VMEM((rows, HEAD), f32), pltpu.VMEM((rows, 8, HEAD), f32), pltpu.VMEM((rows, HEAD), f32), pltpu.VMEM((2, rows, 16, HEAD), bf),
            dma((2, rows // GROUP_ROWS)), dma((2,)),
        ],
        compiler_params=pltpu.CompilerParams(vmem_limit_bytes=ATTN_LIMIT),
    )(seq_lens, projected, b_q, b_k, b_v, freq, k_cache.reshape(rows, seq, HEAD), v_cache.reshape(rows, seq, HEAD))


def solution(mesh):
    mx_size = mesh.shape["mx"]
    act_spec = P(None, "mx")
    cache_spec = P("mx", None, "my", None)
    in_specs = (act_spec, P("mx"), P("mx"), P("mx"), P("mx", "my"), P("my"), P("mx", "my"), P("my"), P("mx", "my"), P("my"), P("my", "mx"), P("mx", "my"), P("mx", "my"), P("my", "mx"), cache_spec, cache_spec)
    out_specs = (act_spec, cache_spec, cache_spec)

    def local_layer(x_in, seq_lens, gain_attn, gain_mlp, w_q, b_q, w_k, b_k, w_v, b_v, w_o, w_gate, w_up, w_down, k_cache, v_cache):
        hidden = x_in.shape[1] * mx_size
        projected = qkv_call(x_in, gain_attn, w_q, w_k, w_v, hidden)
        attn_rows, k_out, v_out = attn_call(seq_lens, projected, b_q, b_k, b_v, k_cache, v_cache)
        pieces = mlp_call(x_in, gain_mlp, attn_rows, w_o, w_gate.T, w_up.T, w_down, hidden)
        x_out = place_call(pieces, x_in.shape)
        k_cache_out, v_cache_out = k_out.reshape(k_cache.shape), v_out.reshape(v_cache.shape)
        return x_out, k_cache_out, v_cache_out

    return jax.shard_map(local_layer, mesh=mesh, in_specs=in_specs, out_specs=out_specs, check_vma=False)
```

profile of v0, /device:TPU:0, one launch (start us, length us, event | category | flops | bytes accessed | tf_op | source)
XLA Modules:
  0.0 87.3 jit_solution(6374208472912744284)
XLA Ops:
  0.6 0.0 copy-start
  0.6 0.0 copy-start.1
  0.7 0.0 copy-start.5
  0.7 0.0 copy-start.6
  0.7 0.0 copy-start.7
  0.7 0.0 copy-start.8
  0.7 0.0 copy-start.9
  0.7 11.6 %qkv.1.proj_ref = f32[48,896]{1,0:T(8,128)S(1)} custom-call(bf16[192,1280]{1,0:T(8,128)(2,1)} %x_v.1, bf16[1280]{0:T(1024)(128)(2,1)} %gain_hbm.1, bf16[1280,640]{1,0:T(8,128)(2,1)} %wq_hbm.1, bf16[1280,128]{1,0:T(8,128)(2,1)} %wk_hbm.1, bf16[1280,128]{1,0:T(8,128)(2,1)} %wv_hbm.1), custom_call_target="tpu_custom_call" | custom-call | flops 10000000000 | bytes 3000000 | tf_op jit(solution)/shard_map/qkv/pallas_call | solution.py:126
  12.3 0.0 copy-done
  12.3 0.0 copy-done.1
  12.3 0.0 copy-done.5
  12.3 0.0 copy-done.6
  12.3 0.0 copy-done.7
  12.3 0.0 copy-done.8
  12.4 0.0 copy-done.9
  12.4 0.0 copy-start.2
  12.4 0.0 copy-start.3
  12.4 0.0 copy-start.4
  12.4 5.0 %attn.1 = (bf16[48,640]{1,0:T(8,128)(2,1)S(1)}, bf16[48,384,128]{2,1,0:T(8,128)(2,1)}, bf16[48,384,128]{2,1,0:T(8,128)(2,1)}) custom-call(s32[48]{0:T(128)S(1)} %copy-done.6, f32[48,896]{1,0:T(8,128)S(1)} %qkv.1.proj_ref, bf16[640]{0:T(1024)(128)(2,1)S(1)} %copy-done.5, bf16[128]{0:T(256)(128)(2,1)S(1)} %copy-done.7, bf16[128]{0:T(256)(128)(2,1)S(1)} %copy-done.8, ...), custom_call_target="tpu_custom_call" | custom-call | tf_op jit(solution)/shard_map/attn/pallas_call | solution.py:611
  17.4 0.0 copy-done.2
  17.4 0.0 copy-done.3
  17.4 0.0 copy-done.4
  17.4 69.0 %mlp.1.pieces_ref = bf16[3,8,16,640]{3,2,1,0:T(8,128)(2,1)S(1)} custom-call(bf16[192,1280]{1,0:T(8,128)(2,1)S(1)} %copy-done.3, bf16[1280]{0:T(1024)(128)(2,1)S(1)} %copy-done.4, bf16[48,640]{1,0:T(8,128)(2,1)S(1)} %get-tuple-element.6.attn_ref, bf16[640,1280]{1,0:T(8,128)(2,1)S(1)} %copy-done.2, bf16[3424,1280]{1,0:T(8,128)(2,1)} %bitcast.12, ...), custom_call_target="tpu_custom_call" | custom-call | tf_op jit(solution)/shard_map/mlp/pallas_call | solution.py:476
  86.5 0.8 place.1
Async XLA Ops:
  0.6 11.7 %copy-start = (bf16[48,384,1,128]{3,1,2,0:T(8,128)(2,1)S(1)}, bf16[48,384,1,128]{3,1,2,0:T(8,128)(2,1)}, u32[]{:S(2)}) copy-start(bf16[48,384,1,128]{3,1,2,0:T(8,128)(2,1)} %param.31) | copy-start | bytes 14155780
  0.6 11.7 %copy-start.1 = (bf16[48,384,1,128]{3,1,2,0:T(8,128)(2,1)S(1)}, bf16[48,384,1,128]{3,1,2,0:T(8,128)(2,1)}, u32[]{:S(2)}) copy-start(bf16[48,384,1,128]{3,1,2,0:T(8,128)(2,1)} %param.32) | copy-start | bytes 14155780
  0.7 11.7 %copy-start.5 = (bf16[640]{0:T(1024)(128)(2,1)S(1)}, bf16[640]{0:T(1024)(128)(2,1)}, u32[]{:S(2)}) copy-start(bf16[640]{0:T(1024)(128)(2,1)} %bq_ref.1) | copy-start | bytes 3844
  0.7 11.7 %copy-start.6 = (s32[48]{0:T(128)S(1)}, s32[48]{0:T(128)}, u32[]{:S(2)}) copy-start(s32[48]{0:T(128)} %seq_ref.1) | copy-start | bytes 580
  0.7 11.7 %copy-start.7 = (bf16[128]{0:T(256)(128)(2,1)S(1)}, bf16[128]{0:T(256)(128)(2,1)}, u32[]{:S(2)}) copy-start(bf16[128]{0:T(256)(128)(2,1)} %bk_ref.1) | copy-start | bytes 772
  0.7 11.7 %copy-start.8 = (bf16[128]{0:T(256)(128)(2,1)S(1)}, bf16[128]{0:T(256)(128)(2,1)}, u32[]{:S(2)}) copy-start(bf16[128]{0:T(256)(128)(2,1)} %bv_ref.1) | copy-start | bytes 772
  0.7 11.7 %copy-start.9 = (f32[1,128]{1,0:T(1,128)S(1)}, f32[1,128]{1,0:T(1,128)}, u32[]{:S(2)}) copy-start(f32[1,128]{1,0:T(1,128)} %constant.2.clone.freq_ref) | copy-start | bytes 1540
  12.4 5.0 %copy-start.2 = (bf16[640,1280]{1,0:T(8,128)(2,1)S(1)}, bf16[640,1280]{1,0:T(8,128)(2,1)}, u32[]{:S(2)}) copy-start(bf16[640,1280]{1,0:T(8,128)(2,1)} %wo_v.1) | copy-start | bytes 4915204
  12.4 5.0 %copy-start.3 = (bf16[192,1280]{1,0:T(8,128)(2,1)S(1)}, bf16[192,1280]{1,0:T(8,128)(2,1)}, u32[]{:S(2)}) copy-start(bf16[192,1280]{1,0:T(8,128)(2,1)} %x_v.1) | copy-start | bytes 1474564
  12.4 5.0 %copy-start.4 = (bf16[1280]{0:T(1024)(128)(2,1)S(1)}, bf16[1280]{0:T(1024)(128)(2,1)}, u32[]{:S(2)}) copy-start(bf16[1280]{0:T(1024)(128)(2,1)} %gain_ref.1) | copy-start | bytes 7684
where the time goes:
time: 87.4 us; the launch traced here: 87.3 us
  Pallas kernels  86.4 us (99%)
    pallas_call x1, Pallas kernels, mlp_call(): pl.pallas_call(functools.partial(mlp_kernel, hidden), name='mlp', out_sha...  69 us
    pallas_call x1, Pallas kernels, qkv_call(): pl.pallas_call(functools.partial(qkv_kernel, hidden), name='qkv', out_sha...  11.6 us
    pallas_call x1, Pallas kernels, attn_call(): pl.pallas_call(attn_kernel, name='attn', out_shape=(jax.ShapeDtypeStruct(...  4.97 us

commit v1 on v0

--- a/solution.py
+++ b/solution.py
@@ -17,7 +17,7 @@
 TILE = 256
 DIRECT = 2
 ROWS = 64
-LAG_B, LAG_C, LAG_D, LAG_E, LAG_M, LAG_F = 1, 4, 7, 8, 3, 9
+LAG_B, LAG_C, LAG_D, LAG_E, LAG_M, LAG_F = 1, 4, 7, 8, 4, 8
 VMEM_LIMIT = 67043328
 MLP_LIMIT = 48 * 1024 * 1024
 ATTN_LIMIT = 14 * 1024 * 1024
@@ -143,9 +143,9 @@
 
 
 def mlp_kernel(hidden, x_v, gain_ref, attn_ref, wo_v, wg_hbm, wu_hbm, wd_hbm, ag2,
-               wg_v, wu_v, wd_v, attn_v, p1, yb1, zs1, zb1, mp, ag1, st_own, st_in, st_sum, st_all, h2,
-               pp, dr, own, xs, xr, act, dacc, p2, yb2, zs2, zb2, mo, eye,
-               ld_sem, send_sem, at_sem, st_sem, sg_sem, ysem1, zsem1, agz1, agy1, ysem2, zsem2, agz2, agy2, d_sem, x_sem, ax_sem, ad_sem, af_sem):
+               wg_v, wu_v, wd_v, attn_v, p1, yb1, zs1, zb1, db1, mp, ag1, st_own, st_in, st_sum, st_all, h2,
+               pp, dr, own, xs, xr, act, dacc, p2, yb2, zs2, zb2, db2, mo, eye,
+               ld_sem, send_sem, at_sem, st_sem, sg_sem, ysem1, zsem1, agz1, agy1, ysem2, zsem2, agz2, agy2, dsem, d_sem, x_sem, ax_sem, ad_sem, af_sem):
     my, mx = lax.axis_index("my"), lax.axis_index("mx")
     n_my = 8
     xi, ci = mx // 2, mx % 2
@@ -199,68 +199,65 @@
             for z in range(4):
                 p1[h, 2 * z + y] = r[16 * z:16 * z + 16]
 
-    parts = ((0, TILE), (TILE, half))
-    spans = [pl.ds(lo, hi - lo) for lo, hi in parts]
-
     def rs_start(r, h):
-        for i, cols in enumerate(spans):
-            for k, z in enumerate(zs):
-                rcopy(r.part.at[h, 2 * z + 1 - yi, :, cols], r.ybuf.at[h, k, :, cols], send_sem.at[r.sem], r.ysem.at[h, i, k], y_dev).start()
-
-    def wait_y(r, h, i, k):
-        got = r.ybuf.at[h, k, :, spans[i]]
-        rcopy(got, got, send_sem.at[r.sem], r.ysem.at[h, i, k], y_dev).wait_recv()
+        for k, z in enumerate(zs):
+            rcopy(r.part.at[h, 2 * z + 1 - yi], r.ybuf.at[h, k], send_sem.at[r.sem], r.ysem.at[h, k], y_dev).start()
+
+    def wait_y(r, h, k):
+        rcopy(r.ybuf.at[h, k], r.ybuf.at[h, k], send_sem.at[r.sem], r.ysem.at[h, k], y_dev).wait_recv()
 
     def rs_mid(r, h):
-        for i, (lo, hi) in enumerate(parts):
-            for k in range(3):
-                wait_y(r, h, i, k)
-                r.zsend[h, k, :, lo:hi] = (r.part[h, 2 * zs[k] + yi, :, lo:hi].astype(f32) + r.ybuf[h, k, :, lo:hi].astype(f32)).astype(bf)
-                rcopy(r.zsend.at[h, k, :, spans[i]], r.zbuf.at[h, k, :, spans[i]], send_sem.at[r.sem + 1], r.zsem.at[h, i], z_devs[k]).start()
-
-    def rs_fin(r, h, i, base):
-        lo, hi = parts[i]
-        wait_y(r, h, i, 3)
-        got = r.zbuf.at[h, :, :, spans[i]]
-        rcopy(got, got, send_sem.at[r.sem + 1], r.zsem.at[h, i], y_dev).wait_recv()
-        total = r.part[h, my, :, lo:hi].astype(f32) + r.ybuf[h, 3, :, lo:hi].astype(f32)
         for k in range(3):
-            total += r.zbuf[h, k, :, lo:hi].astype(f32)
+            wait_y(r, h, k)
+            r.zsend[h, k] = (r.part[h, 2 * zs[k] + yi].astype(f32) + r.ybuf[h, k].astype(f32)).astype(bf)
+            rcopy(r.zsend.at[h, k], r.zbuf.at[h, k], send_sem.at[r.sem + 1], r.zsem.at[h], z_devs[k]).start()
+
+    def rs_fin(r, h, base):
+        wait_y(r, h, 3)
+        rcopy(r.zbuf.at[h], r.zbuf.at[h], send_sem.at[r.sem + 1], r.zsem.at[h], y_dev).wait_recv()
+        total = r.part[h, my].astype(f32) + r.ybuf[h, 3].astype(f32)
+        for k in range(3):
+            total += r.zbuf[h, k].astype(f32)
         return (base + total).astype(bf)
 
-    def ag_start(r, h, i, val):
-        lo, hi = parts[i]
-        r.piece[h, :, lo:hi] = val
-        r.all[h, my, :, lo:hi] = val
-        src, dst = r.piece.at[h, :, spans[i]], r.all.at[h, my, :, spans[i]]
+    def direct_start(r, h):
+        for k, peer in enumerate(peers):
+            rcopy(r.part.at[h, peer], r.dbuf.at[k], send_sem.at[2], r.dsem, {"my": peer}).start()
+
+    def direct_fin(r, h, base):
+        rcopy(r.dbuf, r.dbuf, send_sem.at[2], r.dsem, y_dev).wait_recv()
+        total = r.part[h, my].astype(f32)
+        for k in range(n_my - 1):
+            total += r.dbuf[k].astype(f32)
+        return (base + total).astype(bf)
+
+    def ag_start(r, h, val):
+        r.piece[h] = val
+        r.all[h, my] = val
         for k in range(3):
-            rcopy(src, dst, send_sem.at[r.sem + 2], r.agz.at[h, i, k], z_devs[k]).start()
-        rcopy(src, dst, send_sem.at[r.sem + 2], r.agy.at[h, i], y_dev).start()
+            rcopy(r.piece.at[h], r.all.at[h, my], send_sem.at[r.sem + 2], r.agz.at[h, k], z_devs[k]).start()
+        rcopy(r.piece.at[h], r.all.at[h, my], send_sem.at[r.sem + 2], r.agy.at[h], y_dev).start()
 
     def ag_mid(r, h):
-        for i in range(2):
-            for k in (2, 1, 0):
-                got = r.all.at[h, 2 * zs[k] + yi, :, spans[i]]
-                rcopy(got, got, send_sem.at[r.sem + 2], r.agz.at[h, i, k], y_dev).wait_recv()
-                rcopy(got, got, send_sem.at[r.sem + 2], r.agy.at[h, i], y_dev).start()
+        for k in (2, 1, 0):
+            got = r.all.at[h, 2 * zs[k] + yi]
+            rcopy(got, got, send_sem.at[r.sem + 2], r.agz.at[h, k], y_dev).wait_recv()
+            rcopy(got, got, send_sem.at[r.sem + 2], r.agy.at[h], y_dev).start()
 
     def ag_fin(r, h):
-        for i in range(2):
-            four = r.all.at[h, pl.ds(0, 4), :, spans[i]]
-            rcopy(four, four, send_sem.at[r.sem + 2], r.agy.at[h, i], y_dev).wait_recv()
-
-    one = types.SimpleNamespace(part=p1, ybuf=yb1, zsend=zs1, zbuf=zb1, piece=mp, all=ag1, ysem=ysem1, zsem=zsem1, agz=agz1, agy=agy1, sem=9)
-    two = types.SimpleNamespace(part=p2, ybuf=yb2, zsend=zs2, zbuf=zb2, piece=mo, all=ag2, ysem=ysem2, zsem=zsem2, agz=agz2, agy=agy2, sem=12)
-
-    def rs1_finish(h):
+        four = r.all.at[h, pl.ds(0, 4)]
+        rcopy(four, four, send_sem.at[r.sem + 2], r.agy.at[h], y_dev).wait_recv()
+
+    one = types.SimpleNamespace(part=p1, ybuf=yb1, zsend=zs1, zbuf=zb1, piece=mp, all=ag1, ysem=ysem1, zsem=zsem1, agz=agz1, agy=agy1, dbuf=db1, dsem=dsem.at[0], sem=9)
+    two = types.SimpleNamespace(part=p2, ybuf=yb2, zsend=zs2, zbuf=zb2, piece=mo, all=ag2, ysem=ysem2, zsem=zsem2, agz=agz2, agy=agy2, dbuf=db2, dsem=dsem.at[1], sem=12)
+
+    def rs1_finish(h, fin=rs_fin):
         r0 = pl.multiple_of(zi * brows + h * 16, 16)
-        ss = jnp.zeros((16, 1), f32)
-        for i, (lo, hi) in enumerate(parts):
-            base = x_v[pl.ds(r0, 16), pl.ds(pl.multiple_of(yi * half + lo, 128), hi - lo)].astype(f32)
-            m = rs_fin(one, h, i, base)
-            ag_start(one, h, i, m)
-            m = m.astype(f32)
-            ss += jnp.sum(m * m, axis=1, keepdims=True)
+        base = x_v[pl.ds(r0, 16), pl.ds(pl.multiple_of(yi * half, 128), half)].astype(f32)
+        m = fin(one, h, base)
+        ag_start(one, h, m)
+        m = m.astype(f32)
+        ss = jnp.sum(m * m, axis=1, keepdims=True)
         tile = pack_column([ss[:8], ss[8:]])
         st_own[h] = tile
         st_in[h, mx] = tile
@@ -347,38 +344,40 @@
         for z in range(4):
             for y in range(2):
                 p2[h, 2 * z + y] = dacc[h, 16 * z:16 * z + 16, y * half:(y + 1) * half].astype(bf)
-        rs_start(two, h)
-
-    def rs2_finish(h):
-        for i, (lo, hi) in enumerate(parts):
-            ag_start(two, h, i, rs_fin(two, h, i, mp[h, :, lo:hi].astype(f32)))
+
+        @pl.when(h < n_h - 1)
+        def _():
+            rs_start(two, h)
+
+        @pl.when(h == n_h - 1)
+        def _():
+            direct_start(two, h)
+
+    def rs2_finish(h, fin=rs_fin):
+        ag_start(two, h, fin(two, h, mp[h].astype(f32)))
 
     n_t = n_j * (CHUNK // TILE)
     def flip(lo, hi):
         lax.fori_loop(lo, hi, transpose, 0)
 
     project(0)
-    rs_start(one, 0)
+    direct_start(one, 0)
     project(1)
     rs_start(one, 1)
     project(2)
     for ld in loads[:-1]:
         ld.wait()
-    flip(0, 2)
-    rs_mid(one, 0)
-    flip(2, 5)
+    flip(0, 6)
+    rs1_finish(0, direct_fin)
     rs_mid(one, 1)
-    flip(5, 8)
-    rs1_finish(0)
     rs_start(one, 2)
-    flip(8, 10)
-    rs1_finish(1)
+    flip(6, 10)
     stat_gather(0)
     flip(10, 12)
+    ag_mid(one, 0)
+    rs1_finish(1)
     rs_mid(one, 2)
-    ag_mid(one, 0)
     flip(12, n_t)
-    stat_gather(1)
     norm(0)
 
     def body(t, carry):
@@ -390,15 +389,16 @@
         def _():
             norm(2)
 
-        @pl.when(t == 1)
-        def _():
+        @pl.when(t == 2)
+        def _():
+            stat_gather(1)
             ag_mid(one, 1)
 
-        @pl.when(t == 2)
+        @pl.when(t == 3)
         def _():
             rs1_finish(2)
 
-        @pl.when(t == 5)
+        @pl.when(t == 6)
         def _():
             stat_gather(2)
 
@@ -449,17 +449,16 @@
 
     total_t = steps + LAG_E
     lax.fori_loop(0, total_t, body, 0)
-    rs_mid(two, 2)
+    ag_mid(two, 0)
     rs2_finish(1)
-    ag_mid(two, 0)
-    rs2_finish(2)
+    rs2_finish(2, direct_fin)
     ag_mid(two, 1)
     ag_mid(two, 2)
     for h in range(n_h):
         ag_fin(two, h)
     seven = pl.ds(0, n_my - 1)
     for k, ref in ((0, attn_v.at[:, pl.ds(0, 48)]), (1, st_all.at[:, seven]), (3, st_in.at[:, pl.ds(0, 3)]), (4, dr), (5, xs), (6, act.at[:, 0]), (7, act.at[:, 0]), (8, act.at[:, 0]),
-                   (9, yb1), (10, zb1), (11, ag1.at[:, seven]), (12, yb2), (13, zb2), (14, ag2.at[:, seven])):
+                   (9, yb1.at[pl.ds(1, n_h - 1)]), (10, zb1.at[pl.ds(1, n_h - 1)]), (11, ag1.at[:, seven]), (12, yb2.at[pl.ds(0, n_h - 1)]), (13, zb2.at[pl.ds(0, n_h - 1)]), (2, db1), (2, db2), (14, ag2.at[:, seven])):
         rcopy(ref, ref, send_sem.at[k], at_sem.at[0], core_dev).wait_send()
 
 
@@ -482,13 +481,13 @@
         scratch_shapes=[
             pltpu.VMEM((cols // TILE, n_j * CHUNK, TILE), bf), pltpu.VMEM((cols // TILE, n_j * CHUNK, TILE), bf),
             pltpu.VMEM((n_j * CHUNK, cols), bf), pltpu.VMEM((n_h, 64, attn.shape[1]), bf),
-            pltpu.VMEM((n_h, 8, 16, half), bf), pltpu.VMEM((n_h, 4, 16, half), bf), pltpu.VMEM((n_h, 3, 16, half), bf), pltpu.VMEM((n_h, 3, 16, half), bf), pltpu.VMEM((n_h, 16, half), bf), pltpu.VMEM((n_h, 8, 16, half), bf),
+            pltpu.VMEM((n_h, 8, 16, half), bf), pltpu.VMEM((n_h, 4, 16, half), bf), pltpu.VMEM((n_h, 3, 16, half), bf), pltpu.VMEM((n_h, 3, 16, half), bf), pltpu.VMEM((7, 16, half), bf), pltpu.VMEM((n_h, 16, half), bf), pltpu.VMEM((n_h, 8, 16, half), bf),
             pltpu.VMEM((n_h, 8, 128), f32), pltpu.VMEM((n_h, 4, 8, 128), f32), pltpu.VMEM((n_h, 8, 128), f32), pltpu.VMEM((n_h, 8, 8, 128), f32), pltpu.VMEM((n_h, ROWS, cols), bf),
             pltpu.VMEM((steps, 2, 2, 16, 2 * CHUNK), bf), pltpu.VMEM((steps, 2, 16, 2 * CHUNK), bf), pltpu.VMEM((steps, 16, 2 * CHUNK), f32),
             pltpu.VMEM((steps, 16, 2 * CHUNK), bf), pltpu.VMEM((steps, 16, 2 * CHUNK), bf), pltpu.VMEM((steps, 4, 16, CHUNK), bf),
             pltpu.VMEM((n_h, ROWS, cols), f32),
-            pltpu.VMEM((n_h, 8, 16, half), bf), pltpu.VMEM((n_h, 4, 16, half), bf), pltpu.VMEM((n_h, 3, 16, half), bf), pltpu.VMEM((n_h, 3, 16, half), bf), pltpu.VMEM((n_h, 16, half), bf), pltpu.VMEM((TILE, TILE), bf),
-            dma((1 + 2 * (cols // TILE),)), dma((15,)), dma((n_h,)), dma((n_h,)), dma((n_h,)), dma((n_h, 2, 4)), dma((n_h, 2)), dma((n_h, 2, 3)), dma((n_h, 2)), dma((n_h, 2, 4)), dma((n_h, 2)), dma((n_h, 2, 3)), dma((n_h, 2)),
+            pltpu.VMEM((n_h, 8, 16, half), bf), pltpu.VMEM((n_h, 4, 16, half), bf), pltpu.VMEM((n_h, 3, 16, half), bf), pltpu.VMEM((n_h, 3, 16, half), bf), pltpu.VMEM((7, 16, half), bf), pltpu.VMEM((n_h, 16, half), bf), pltpu.VMEM((TILE, TILE), bf),
+            dma((1 + 2 * (cols // TILE),)), dma((15,)), dma((n_h,)), dma((n_h,)), dma((n_h,)), dma((n_h, 4)), dma((n_h,)), dma((n_h, 3)), dma((n_h,)), dma((n_h, 4)), dma((n_h,)), dma((n_h, 3)), dma((n_h,)), dma((2,)),
             dma((steps,)), dma((steps,)), dma((steps,)), dma((steps,)), dma((steps,)),
         ],
         compiler_params=pltpu.CompilerParams(collective_id=1, has_side_effects=True, vmem_limit_bytes=MLP_LIMIT),

time: 87.4 us -> 85 us (0.973)
  Pallas kernels: 86.4 us -> 84 us
    pallas_call x1, Pallas kernels: 69 us -> 66.6 us  [mlp_call(): pl.pallas_call(functools.partial(mlp_kernel, hidden), name='mlp', out_sha...]
where the time goes in v1:
time: 85 us; the launch traced here: 84.8 us
  Pallas kernels  84 us (99%)
    pallas_call x1, Pallas kernels, mlp_call(): pl.pallas_call(functools.partial(mlp_kernel, hidden), name='mlp', out_sha...  66.6 us
    pallas_call x1, Pallas kernels, qkv_call(): pl.pallas_call(functools.partial(qkv_kernel, hidden), name='qkv', out_sha...  11.6 us
    pallas_call x1, Pallas kernels, attn_call(): pl.pallas_call(attn_kernel, name='attn', out_shape=(jax.ShapeDtypeStruct(...  4.97 us

profile of v1, /device:TPU:0, one launch (start us, length us, event | category | flops | bytes accessed | tf_op | source)
XLA Modules:
  0.0 84.8 jit_solution(10798861588246924174)
XLA Ops:
  0.6 0.0 copy-start
  0.6 0.0 copy-start.1
  0.7 0.0 copy-start.5
  0.7 0.0 copy-start.6
  0.7 0.0 copy-start.7
  0.7 0.0 copy-start.8
  0.7 0.0 copy-start.9
  0.7 11.6 %qkv.1.proj_ref = f32[48,896]{1,0:T(8,128)S(1)} custom-call(bf16[192,1280]{1,0:T(8,128)(2,1)} %x_v.1, bf16[1280]{0:T(1024)(128)(2,1)} %gain_hbm.1, bf16[1280,640]{1,0:T(8,128)(2,1)} %wq_hbm.1, bf16[1280,128]{1,0:T(8,128)(2,1)} %wk_hbm.1, bf16[1280,128]{1,0:T(8,128)(2,1)} %wv_hbm.1), custom_call_target="tpu_custom_call" | custom-call | flops 10000000000 | bytes 3000000 | tf_op jit(solution)/shard_map/qkv/pallas_call | solution.py:126
  12.3 0.0 copy-done
  12.3 0.0 copy-done.1
  12.3 0.0 copy-done.5
  12.3 0.0 copy-done.6
  12.3 0.0 copy-done.7
  12.3 0.0 copy-done.8
  12.4 0.0 copy-done.9
  12.4 0.0 copy-start.2
  12.4 0.0 copy-start.3
  12.4 0.0 copy-start.4
  12.4 5.0 %attn.1 = (bf16[48,640]{1,0:T(8,128)(2,1)S(1)}, bf16[48,384,128]{2,1,0:T(8,128)(2,1)}, bf16[48,384,128]{2,1,0:T(8,128)(2,1)}) custom-call(s32[48]{0:T(128)S(1)} %copy-done.6, f32[48,896]{1,0:T(8,128)S(1)} %qkv.1.proj_ref, bf16[640]{0:T(1024)(128)(2,1)S(1)} %copy-done.5, bf16[128]{0:T(256)(128)(2,1)S(1)} %copy-done.7, bf16[128]{0:T(256)(128)(2,1)S(1)} %copy-done.8, ...), custom_call_target="tpu_custom_call" | custom-call | tf_op jit(solution)/shard_map/attn/pallas_call | solution.py:610
  17.4 0.0 copy-done.2
  17.4 0.0 copy-done.3
  17.4 0.0 copy-done.4
  17.4 66.6 %mlp.1.pieces_ref = bf16[3,8,16,640]{3,2,1,0:T(8,128)(2,1)S(1)} custom-call(bf16[192,1280]{1,0:T(8,128)(2,1)S(1)} %copy-done.3, bf16[1280]{0:T(1024)(128)(2,1)S(1)} %copy-done.4, bf16[48,640]{1,0:T(8,128)(2,1)S(1)} %get-tuple-element.6.attn_ref, bf16[640,1280]{1,0:T(8,128)(2,1)S(1)} %copy-done.2, bf16[3424,1280]{1,0:T(8,128)(2,1)} %bitcast.12, ...), custom_call_target="tpu_custom_call" | custom-call | tf_op jit(solution)/shard_map/mlp/pallas_call | solution.py:475
  84.0 0.8 place.1
Async XLA Ops:
  0.6 11.7 %copy-start = (bf16[48,384,1,128]{3,1,2,0:T(8,128)(2,1)S(1)}, bf16[48,384,1,128]{3,1,2,0:T(8,128)(2,1)}, u32[]{:S(2)}) copy-start(bf16[48,384,1,128]{3,1,2,0:T(8,128)(2,1)} %param.31) | copy-start | bytes 14155780
  0.6 11.7 %copy-start.1 = (bf16[48,384,1,128]{3,1,2,0:T(8,128)(2,1)S(1)}, bf16[48,384,1,128]{3,1,2,0:T(8,128)(2,1)}, u32[]{:S(2)}) copy-start(bf16[48,384,1,128]{3,1,2,0:T(8,128)(2,1)} %param.32) | copy-start | bytes 14155780
  0.7 11.7 %copy-start.5 = (bf16[640]{0:T(1024)(128)(2,1)S(1)}, bf16[640]{0:T(1024)(128)(2,1)}, u32[]{:S(2)}) copy-start(bf16[640]{0:T(1024)(128)(2,1)} %bq_ref.1) | copy-start | bytes 3844
  0.7 11.7 %copy-start.6 = (s32[48]{0:T(128)S(1)}, s32[48]{0:T(128)}, u32[]{:S(2)}) copy-start(s32[48]{0:T(128)} %seq_ref.1) | copy-start | bytes 580
  0.7 11.7 %copy-start.7 = (bf16[128]{0:T(256)(128)(2,1)S(1)}, bf16[128]{0:T(256)(128)(2,1)}, u32[]{:S(2)}) copy-start(bf16[128]{0:T(256)(128)(2,1)} %bk_ref.1) | copy-start | bytes 772
  0.7 11.7 %copy-start.8 = (bf16[128]{0:T(256)(128)(2,1)S(1)}, bf16[128]{0:T(256)(128)(2,1)}, u32[]{:S(2)}) copy-start(bf16[128]{0:T(256)(128)(2,1)} %bv_ref.1) | copy-start | bytes 772
  0.7 11.7 %copy-start.9 = (f32[1,128]{1,0:T(1,128)S(1)}, f32[1,128]{1,0:T(1,128)}, u32[]{:S(2)}) copy-start(f32[1,128]{1,0:T(1,128)} %constant.2.clone.freq_ref) | copy-start | bytes 1540
  12.4 5.0 %copy-start.2 = (bf16[640,1280]{1,0:T(8,128)(2,1)S(1)}, bf16[640,1280]{1,0:T(8,128)(2,1)}, u32[]{:S(2)}) copy-start(bf16[640,1280]{1,0:T(8,128)(2,1)} %wo_v.1) | copy-start | bytes 4915204
  12.4 5.0 %copy-start.3 = (bf16[192,1280]{1,0:T(8,128)(2,1)S(1)}, bf16[192,1280]{1,0:T(8,128)(2,1)}, u32[]{:S(2)}) copy-start(bf16[192,1280]{1,0:T(8,128)(2,1)} %x_v.1) | copy-start | bytes 1474564
  12.4 5.0 %copy-start.4 = (bf16[1280]{0:T(1024)(128)(2,1)S(1)}, bf16[1280]{0:T(1024)(128)(2,1)}, u32[]{:S(2)}) copy-start(bf16[1280]{0:T(1024)(128)(2,1)} %gain_ref.1) | copy-start | bytes 7684

commit v2 on v1

--- a/solution.py
+++ b/solution.py
@@ -494,21 +494,34 @@
     )(x_in, gain, attn, w_o, pinned(w_gate), pinned(w_up), pinned(w_down))
 
 
-def place_kernel(pieces_ref, out_ref):
+def place_kernel(pieces_ref, out_hbm, sem):
     n_h, _, _, half = pieces_ref.shape
+    copies = []
     for h in range(n_h):
         for z in range(4):
             for y in range(2):
                 r0 = z * 16 * n_h + h * 16
-                out_ref[r0:r0 + 16, y * half:(y + 1) * half] = pieces_ref[h, 2 * z + y]
+                dst = out_hbm.at[pl.ds(r0, 16), pl.ds(y * half, half)]
+                copies.append(pltpu.make_async_copy(pieces_ref.at[h, 2 * z + y], dst, sem.at[len(copies)]))
+    for cp in copies:
+        cp.start()
+    for cp in copies:
+        cp.wait()
 
 
 def place_call(pieces, shape):
-    vmem = pl.BlockSpec(memory_space=pltpu.VMEM)
-    return pl.pallas_call(place_kernel, name="place", out_shape=jax.ShapeDtypeStruct(shape, pieces.dtype), in_specs=[vmem], out_specs=vmem, compiler_params=pltpu.CompilerParams(vmem_limit_bytes=4 * 1024 * 1024))(pieces)
-
-
-GROUP_ROWS = 16
+    return pl.pallas_call(
+        place_kernel,
+        name="place",
+        out_shape=jax.ShapeDtypeStruct(shape, pieces.dtype),
+        in_specs=[pl.BlockSpec(memory_space=pltpu.VMEM)],
+        out_specs=pl.BlockSpec(memory_space=pl.ANY),
+        scratch_shapes=[pltpu.SemaphoreType.DMA((pieces.shape[0] * pieces.shape[1],))],
+        compiler_params=pltpu.CompilerParams(vmem_limit_bytes=4 * 1024 * 1024),
+    )(pieces)
+
+
+GROUP_ROWS = 24
 
 
 def attn_kernel(seq_ref, proj_ref, bq_ref, bk_ref, bv_ref, freq_ref, k_ref, v_ref, attn_ref, ko_hbm, vo_hbm, qs, kn, vn, os, pos, patch, out_sem, patch_sem):

time: 85 us -> 85.2 us (level)
  no operation moved by 1% of the time
where the time goes in v2:
time: 85.2 us; the launch traced here: 85.1 us
  Pallas kernels  84.2 us (99%)
    pallas_call x1, Pallas kernels, mlp_call(): pl.pallas_call(functools.partial(mlp_kernel, hidden), name='mlp', out_sha...  66.6 us
    pallas_call x1, Pallas kernels, qkv_call(): pl.pallas_call(functools.partial(qkv_kernel, hidden), name='qkv', out_sha...  11.6 us
    pallas_call x1, Pallas kernels, attn_call(): pl.pallas_call(attn_kernel, name='attn', out_shape=(jax.ShapeDtypeStruct(...  5.04 us

profile of v2, /device:TPU:0, one launch (start us, length us, event | category | flops | bytes accessed | tf_op | source)
XLA Modules:
  0.0 85.1 jit_solution(16269349970971911030)
XLA Ops:
  0.6 0.0 copy-start
  0.6 0.0 copy-start.1
  0.7 0.0 copy-start.5
  0.7 0.0 copy-start.6
  0.7 0.0 copy-start.7
  0.7 0.0 copy-start.8
  0.7 0.0 copy-start.9
  0.7 11.6 %qkv.1.proj_ref = f32[48,896]{1,0:T(8,128)S(1)} custom-call(bf16[192,1280]{1,0:T(8,128)(2,1)} %x_v.1, bf16[1280]{0:T(1024)(128)(2,1)} %gain_hbm.1, bf16[1280,640]{1,0:T(8,128)(2,1)} %wq_hbm.1, bf16[1280,128]{1,0:T(8,128)(2,1)} %wk_hbm.1, bf16[1280,128]{1,0:T(8,128)(2,1)} %wv_hbm.1), custom_call_target="tpu_custom_call" | custom-call | flops 10000000000 | bytes 3000000 | tf_op jit(solution)/shard_map/qkv/pallas_call | solution.py:126
  12.3 0.0 copy-done
  12.3 0.0 copy-done.1
  12.3 0.0 copy-done.5
  12.3 0.0 copy-done.6
  12.3 0.0 copy-done.7
  12.3 0.0 copy-done.8
  12.4 0.0 copy-done.9
  12.4 0.0 copy-start.2
  12.4 0.0 copy-start.3
  12.4 0.0 copy-start.4
  12.4 5.0 %attn.1 = (bf16[48,640]{1,0:T(8,128)(2,1)S(1)}, bf16[48,384,128]{2,1,0:T(8,128)(2,1)}, bf16[48,384,128]{2,1,0:T(8,128)(2,1)}) custom-call(s32[48]{0:T(128)S(1)} %copy-done.6, f32[48,896]{1,0:T(8,128)S(1)} %qkv.1.proj_ref, bf16[640]{0:T(1024)(128)(2,1)S(1)} %copy-done.5, bf16[128]{0:T(256)(128)(2,1)S(1)} %copy-done.7, bf16[128]{0:T(256)(128)(2,1)S(1)} %copy-done.8, ...), custom_call_target="tpu_custom_call" | custom-call | tf_op jit(solution)/shard_map/attn/pallas_call | solution.py:623
  17.4 0.0 copy-done.2
  17.5 0.0 copy-done.3
  17.5 0.0 copy-done.4
  17.5 66.6 %mlp.1.pieces_ref = bf16[3,8,16,640]{3,2,1,0:T(8,128)(2,1)S(1)} custom-call(bf16[192,1280]{1,0:T(8,128)(2,1)S(1)} %copy-done.3, bf16[1280]{0:T(1024)(128)(2,1)S(1)} %copy-done.4, bf16[48,640]{1,0:T(8,128)(2,1)S(1)} %get-tuple-element.6.attn_ref, bf16[640,1280]{1,0:T(8,128)(2,1)S(1)} %copy-done.2, bf16[3424,1280]{1,0:T(8,128)(2,1)} %bitcast.12, ...), custom_call_target="tpu_custom_call" | custom-call | tf_op jit(solution)/shard_map/mlp/pallas_call | solution.py:475
  84.1 1.0 %place.1 = bf16[192,1280]{1,0:T(8,128)(2,1)} custom-call(bf16[3,8,16,640]{3,2,1,0:T(8,128)(2,1)S(1)} %mlp.1.pieces_ref), custom_call_target="tpu_custom_call" | custom-call | tf_op jit(solution)/shard_map/place/pallas_call | solution.py:513
Async XLA Ops:
  0.6 11.7 %copy-start = (bf16[48,384,1,128]{3,1,2,0:T(8,128)(2,1)S(1)}, bf16[48,384,1,128]{3,1,2,0:T(8,128)(2,1)}, u32[]{:S(2)}) copy-start(bf16[48,384,1,128]{3,1,2,0:T(8,128)(2,1)} %param.31) | copy-start | bytes 14155780
  0.6 11.7 %copy-start.1 = (bf16[48,384,1,128]{3,1,2,0:T(8,128)(2,1)S(1)}, bf16[48,384,1,128]{3,1,2,0:T(8,128)(2,1)}, u32[]{:S(2)}) copy-start(bf16[48,384,1,128]{3,1,2,0:T(8,128)(2,1)} %param.32) | copy-start | bytes 14155780
  0.7 11.7 %copy-start.5 = (bf16[640]{0:T(1024)(128)(2,1)S(1)}, bf16[640]{0:T(1024)(128)(2,1)}, u32[]{:S(2)}) copy-start(bf16[640]{0:T(1024)(128)(2,1)} %bq_ref.1) | copy-start | bytes 3844
  0.7 11.7 %copy-start.6 = (s32[48]{0:T(128)S(1)}, s32[48]{0:T(128)}, u32[]{:S(2)}) copy-start(s32[48]{0:T(128)} %seq_ref.1) | copy-start | bytes 580
  0.7 11.7 %copy-start.7 = (bf16[128]{0:T(256)(128)(2,1)S(1)}, bf16[128]{0:T(256)(128)(2,1)}, u32[]{:S(2)}) copy-start(bf16[128]{0:T(256)(128)(2,1)} %bk_ref.1) | copy-start | bytes 772
  0.7 11.7 %copy-start.8 = (bf16[128]{0:T(256)(128)(2,1)S(1)}, bf16[128]{0:T(256)(128)(2,1)}, u32[]{:S(2)}) copy-start(bf16[128]{0:T(256)(128)(2,1)} %bv_ref.1) | copy-start | bytes 772
  0.7 11.7 %copy-start.9 = (f32[1,128]{1,0:T(1,128)S(1)}, f32[1,128]{1,0:T(1,128)}, u32[]{:S(2)}) copy-start(f32[1,128]{1,0:T(1,128)} %constant.2.clone.freq_ref) | copy-start | bytes 1540
  12.4 5.1 %copy-start.2 = (bf16[640,1280]{1,0:T(8,128)(2,1)S(1)}, bf16[640,1280]{1,0:T(8,128)(2,1)}, u32[]{:S(2)}) copy-start(bf16[640,1280]{1,0:T(8,128)(2,1)} %wo_v.1) | copy-start | bytes 4915204
  12.4 5.1 %copy-start.3 = (bf16[192,1280]{1,0:T(8,128)(2,1)S(1)}, bf16[192,1280]{1,0:T(8,128)(2,1)}, u32[]{:S(2)}) copy-start(bf16[192,1280]{1,0:T(8,128)(2,1)} %x_v.1) | copy-start | bytes 1474564
  12.4 5.1 %copy-start.4 = (bf16[1280]{0:T(1024)(128)(2,1)S(1)}, bf16[1280]{0:T(1024)(128)(2,1)}, u32[]{:S(2)}) copy-start(bf16[1280]{0:T(1024)(128)(2,1)} %gain_ref.1) | copy-start | bytes 7684
